TPU v7x, 256 devices: a whole 4x4x8 slice. The times are simulated.
256 devices in a mesh: node: 32 (over y_lo, z, core), local: 8 (over y_hi, x).
Axes of the slice: x: 4, y: 4 (y_hi: 2, y_lo: 2; y = y_hi * 2 + y_lo), z: 8, core: 2. Of those that a mesh axis runs over, the one named last changes fastest.
Arguments:
- activations: bfloat16 [32768, 4096], P(('node', 'local')), may hold values from -24 to 24
- out_grads: bfloat16 [32768, 512], P(('node', 'local')), may hold values from -6 to 6
- master: float32 [4096, 512], P(('node', 'local')), may hold values from -0.15 to 0.15
- first_moment: float32 [4096, 512], P(('node', 'local')), may hold values from -0.6 to 0.6
- second_moment: float32 [4096, 512], P(('node', 'local')), may hold values from 0.01 to 1
Outputs:
- new_weight: bfloat16 [4096, 512], P('node')
- new_first: float32 [4096, 512], P(('node', 'local'))
- new_second: float32 [4096, 512], P(('node', 'local'))
All inputs are finite; a program needn't handle non-finite values.
Results may differ from a plain program's by a relative error of at most 0.009.
Values may be sent and summed in bfloat16 or wider, within the bound.
A program may use at most 128 MiB of HBM per device.

v0:
```python
import jax
import jax.numpy as jnp
from jax import lax
from jax.sharding import PartitionSpec as P

BLOCK = 256


def from_everyone(shard, axis):
    copies = jnp.broadcast_to(shard, (lax.axis_size(axis), *shard.shape))
    return lax.all_to_all(copies, axis, split_axis=0, concat_axis=0, tiled=True)


def joined_along(parts, dim):
    dims = list(parts.shape[1:])
    dims[dim] *= parts.shape[0]
    return jnp.moveaxis(parts, 0, dim).reshape(dims)


def gathered_copies(shard, axis, dim):
    parts = from_everyone(shard, axis)
    return joined_along(parts, dim)


def quantize(values):
    blocks = values.reshape(values.shape[:-1] + (values.shape[-1] // BLOCK, BLOCK))
    largest = jnp.max(jnp.abs(blocks), axis=-1)
    scale = (largest + 1e-06) / 127.0
    payload = (blocks / scale[..., None]).astype(jnp.bfloat16)
    return (payload.reshape(values.shape), scale)


def restore_sum(payload, scale, axis):
    blocks = payload.reshape(payload.shape[:-1] + (scale.shape[-1], BLOCK))
    values = blocks.astype(jnp.float32) * scale[..., None]
    values = values.reshape(payload.shape)
    return jnp.sum(values, axis=axis)


def per_device(activations, out_grads, master, first_moment, second_moment):
    node_count = lax.axis_size("node")
    local_count = lax.axis_size("local")
    own_rows = master.shape[0]
    col_count = master.shape[1]
    token_count = activations.shape[0]
    bands = activations.reshape(token_count, node_count, local_count, own_rows)
    got_inputs = lax.all_to_all(bands, "local", split_axis=2, concat_axis=0, tiled=True)
    got_outputs = gathered_copies(out_grads, "local", 0)
    got_inputs = got_inputs.reshape(local_count, token_count, node_count * own_rows)
    got_outputs = got_outputs.reshape(local_count, token_count, col_count)
    grads = jnp.einsum("ltr,ltk->lrk", got_inputs, got_outputs, preferred_element_type=jnp.float32)
    payload, scale = quantize(grads)
    first_sum = restore_sum(payload, scale, 0).reshape(node_count, own_rows, col_count)
    second_payload, second_scale = quantize(first_sum)
    node_payload, node_scale = (
        lax.all_to_all(second_payload, "node", split_axis=0, concat_axis=0, tiled=True),
        lax.all_to_all(
            second_scale.astype(jnp.bfloat16), "node", split_axis=0, concat_axis=0, tiled=True
        ).astype(second_scale.dtype),
    )
    total = restore_sum(node_payload, node_scale, 0)
    grad_mean = total / (node_count * local_count)
    new_first = 0.9 * first_moment + 0.1 * grad_mean
    new_second = 0.95 * second_moment + 0.05 * grad_mean * grad_mean
    update = new_first / (1.0 - 0.9**10) / (jnp.sqrt(new_second / (1.0 - 0.95**10)) + 1e-08)
    own_weight = (master - 0.01 * update).astype(jnp.bfloat16)
    new_weight = gathered_copies(own_weight, "local", 0)
    return (new_weight, new_first, new_second)


def solution(mesh):
    in_specs = (
        P(("node", "local"), None),
        P(("node", "local"), None),
        P(("node", "local"), None),
        P(("node", "local"), None),
        P(("node", "local"), None),
    )
    out_specs = (P("node", None), P(("node", "local"), None), P(("node", "local"), None))
    return jax.shard_map(
        per_device, mesh=mesh, in_specs=in_specs, out_specs=out_specs, check_vma=False
    )
```

profile of v0, /device:TPU:1, one launch (start us, length us, event | category | flops | bytes accessed | tf_op | source)
XLA Modules:
  0.0 104.9 jit_solution(4332789085037720978)
XLA Ops:
  0.6 1.0 copy.38
  1.7 1.1 %broadcast_in_dim.4 = bf16[8,128,512]{1,2,0:T(8,128)(2,1)} broadcast(bf16[128,512]{0,1:T(8,128)(2,1)S(1)} %copy.38), dimensions={1,2} | broadcast | bytes 1179648 | tf_op jit(solution)/shard_map/broadcast_in_dim | solution.py:10
  2.8 7.5 %all-to-all-start.1 = ((bf16[8,128,512]{1,2,0:T(8,128)(2,1)}), bf16[8,128,512]{1,2,0:T(8,128)(2,1)S(1)}, u32[]{:S(2)}, u32[]{:S(2)}) async-start(bf16[8,128,512]{1,2,0:T(8,128)(2,1)} %broadcast_in_dim.4), calls=%async_computation.1 | async-start | bytes 2097152 | tf_op jit(solution)/shard_map/all_to_all | solution.py:11
  10.3 1.6 %copy.36 = bf16[128,4096]{0,1:T(8,128)(2,1)S(1)} copy(bf16[128,4096]{1,0:T(8,128)(2,1)} %param.5) | data formatting | bytes 2097152 | tf_op args[0]
  11.9 0.2 copy.37
  12.1 15.6 %all-to-all-done.1 = bf16[8,128,512]{1,2,0:T(8,128)(2,1)S(1)} async-done(((bf16[8,128,512]{1,2,0:T(8,128)(2,1)}), bf16[8,128,512]{1,2,0:T(8,128)(2,1)S(1)}, u32[]{:S(2)}, u32[]{:S(2)}) %all-to-all-start.1) | async-done | bytes 1048608 | tf_op jit(solution)/shard_map/all_to_all | solution.py:11
  27.6 18.8 %all_to_all.35 = bf16[128,32,8,16]{0,3,1,2:T(8,128)(2,1)S(1)} all-to-all(bf16[128,32,8,16]{0,3,1,2:T(8,128)(2,1)S(1)} %copy.37), channel_id=1, replica_groups=mesh['node'=32,'local'=8] {'local'}, dimensions={2} | all-to-all | bytes 2097152 | tf_op jit(solution)/shard_map/all_to_all | solution.py:47
  46.4 1.3 %bitcast_reduce_fusion = (f32[8,512,2]{1,2,0:T(2,128)S(1)}, f32[8,512,512]{1,2,0:T(8,128)S(1)}) fusion(bf16[8,128,512]{1,2,0:T(8,128)(2,1)S(1)} %bitcast.21, bf16[8,128,512]{1,2,0:T(8,128)(2,1)S(1)} %all-to-all-done.1), kind=kOutput, calls=%fused_computation.4 | convolution fusion | flops 541057024 | bytes 10518528 | tf_op jit(solution)/shard_map/ltr,ltk->lrk/dot_general | solution.py:51
  47.7 1.2 %fusion.1 = f32[512,512]{0,1:T(8,128)S(1)} fusion(f32[8,512,512]{1,2,0:T(8,128)S(1)} %get-tuple-element.9, f32[8,512,2]{1,2,0:T(2,128)S(1)} %add_multiply_fusion), kind=kLoop, calls=%fused_computation.3 | loop fusion | flops 10223616 | bytes 9469952 | tf_op jit(solution)/shard_map/reduce_sum | solution.py:37
  48.9 0.1 abs.14
  49.0 0.3 copy.40
  49.3 1.3 %copy.41 = f32[512,512]{1,0:T(8,128)} copy(f32[512,512]{0,1:T(8,128)S(1)} %abs.14) | data formatting | bytes 2097152 | tf_op jit(solution)/shard_map/abs | solution.py:27
  50.7 1.9 %abs.15 = f32[32,16,2,256]{3,2,1,0:T(2,128)S(1)} reshape(f32[512,512]{1,0:T(8,128)} %copy.41) | data formatting | bytes 2097152 | tf_op jit(solution)/shard_map/abs | solution.py:27
  52.6 0.6 reduce_max.19
  53.2 0.2 copy.42
  53.4 0.7 copy.44
  54.1 10.6 %all-to-all-start.3 = ((bf16[32,16,2]{1,2,0:T(2,128)(2,1)}), bf16[32,16,2]{1,2,0:T(2,128)(2,1)S(1)}, u32[]{:S(2)}, u32[]{:S(2)}) async-start(bf16[32,16,2]{1,2,0:T(2,128)(2,1)} %copy.44), calls=%async_computation.3 | async-start | bytes 32768 | tf_op jit(solution)/shard_map/all_to_all | solution.py:57
  64.6 0.2 copy.43
  64.8 0.6 div.62
  65.5 0.8 div.63
  66.3 1.0 divide_convert_fusion
  67.3 5.1 %all-to-all-done.3 = bf16[32,16,2]{1,2,0:T(2,128)(2,1)S(1)} async-done(((bf16[32,16,2]{1,2,0:T(2,128)(2,1)}), bf16[32,16,2]{1,2,0:T(2,128)(2,1)S(1)}, u32[]{:S(2)}, u32[]{:S(2)}) %all-to-all-start.3) | async-done | bytes 2080 | tf_op jit(solution)/shard_map/all_to_all | solution.py:57
  72.4 4.4 %all-to-all-start.2 = ((bf16[32,16,512]{2,1,0:T(8,128)(2,1)}), bf16[32,16,512]{2,1,0:T(8,128)(2,1)S(1)}, u32[]{:S(2)}, u32[]{:S(2)}) async-start(bf16[32,16,512]{2,1,0:T(8,128)(2,1)} %divide_convert_fusion), calls=%async_computation.2 | async-start | bytes 1048576 | tf_op jit(solution)/shard_map/all_to_all | solution.py:56
  76.8 0.1 copy.45
  76.9 0.2 copy.46
  77.1 0.6 mul.54
  77.7 0.8 mul.55
  78.5 14.9 %all-to-all-done.2 = bf16[32,16,512]{2,1,0:T(8,128)(2,1)S(1)} async-done(((bf16[32,16,512]{2,1,0:T(8,128)(2,1)}), bf16[32,16,512]{2,1,0:T(8,128)(2,1)S(1)}, u32[]{:S(2)}, u32[]{:S(2)}) %all-to-all-start.2) | async-done | bytes 524320 | tf_op jit(solution)/shard_map/all_to_all | solution.py:56
  93.5 0.2 multiply_reduce_fusion
  93.7 0.6 subtract_convert_fusion
  94.3 9.9 %all_to_all.36 = bf16[8,16,512]{2,1,0:T(8,128)(2,1)S(1)} all-to-all(bf16[8,16,512]{2,1,0:T(8,128)(2,1)S(1)} %broadcast_in_dim.5), channel_id=1, replica_groups=mesh['node'=32,'local'=8] {'local'}, dimensions={0} | all-to-all | bytes 262144 | tf_op jit(solution)/shard_map/all_to_all | solution.py:11
  104.2 0.7 copy.49
  (9 shorter events, 0.1 us)
Async XLA Ops:
  2.8 24.8 %all-to-all-start.1 = ((bf16[8,128,512]{1,2,0:T(8,128)(2,1)}), bf16[8,128,512]{1,2,0:T(8,128)(2,1)S(1)}, u32[]{:S(2)}, u32[]{:S(2)}) async-start(bf16[8,128,512]{1,2,0:T(8,128)(2,1)} %broadcast_in_dim.4), calls=%async_computation.1 | async-start | bytes 2097152 | tf_op jit(solution)/shard_map/all_to_all | solution.py:11
  50.7 43.0 %copy-start = (f32[16,512]{1,0:T(8,128)S(1)}, f32[16,512]{1,0:T(8,128)}, u32[]{:S(2)}) copy-start(f32[16,512]{1,0:T(8,128)} %param.7) | copy-start | bytes 98308
  50.7 43.0 %copy-start.1 = (f32[16,512]{1,0:T(8,128)S(1)}, f32[16,512]{1,0:T(8,128)}, u32[]{:S(2)}) copy-start(f32[16,512]{1,0:T(8,128)} %param.8) | copy-start | bytes 98308
  50.7 43.0 %copy-start.2 = (f32[16,512]{1,0:T(8,128)S(1)}, f32[16,512]{1,0:T(8,128)}, u32[]{:S(2)}) copy-start(f32[16,512]{1,0:T(8,128)} %param.9) | copy-start | bytes 98308
  54.1 18.3 %all-to-all-start.3 = ((bf16[32,16,2]{1,2,0:T(2,128)(2,1)}), bf16[32,16,2]{1,2,0:T(2,128)(2,1)S(1)}, u32[]{:S(2)}, u32[]{:S(2)}) async-start(bf16[32,16,2]{1,2,0:T(2,128)(2,1)} %copy.44), calls=%async_computation.3 | async-start | bytes 32768 | tf_op jit(solution)/shard_map/all_to_all | solution.py:57
  72.4 21.1 %all-to-all-start.2 = ((bf16[32,16,512]{2,1,0:T(8,128)(2,1)}), bf16[32,16,512]{2,1,0:T(8,128)(2,1)S(1)}, u32[]{:S(2)}, u32[]{:S(2)}) async-start(bf16[32,16,512]{2,1,0:T(8,128)(2,1)} %divide_convert_fusion), calls=%async_computation.2 | async-start | bytes 1048576 | tf_op jit(solution)/shard_map/all_to_all | solution.py:56
where the time goes:
time: 107 us; the launch traced here: 105 us
  waiting for transfers between devices  35.6 us (33%)
  blocking collectives  28.6 us (27%)
  starting transfers between devices  22.4 us (21%)
  local copies, waits for them, and re-layouts  12.4 us (12%)
  other arithmetic  3.73 us (3%)
  matrix products  1.3 us (1%)
    all_to_all x1, blocking collectives, per_device(): lax.all_to_all(bands, 'local', split_axis=2, concat_axis=0, tiled=True)  18.8 us
    all_to_all x1, waiting for transfers between devices, from_everyone(): return lax.all_to_all(copies, axis, split_axis=0, concat_axis=0, tiled=True)  15.6 us
    all_to_all x1, waiting for transfers between devices, per_device(): lax.all_to_all(second_payload, 'node', split_axis=0, concat_axis=0, tiled...  14.9 us
    all_to_all x1, starting transfers between devices, per_device(): lax.all_to_all(second_scale.astype(jnp.bfloat16), 'node', split_axis=0, c...  10.6 us
    all_to_all x1, blocking collectives, from_everyone(): return lax.all_to_all(copies, axis, split_axis=0, concat_axis=0, tiled=True)  9.88 us
    all_to_all x1, starting transfers between devices, from_everyone(): return lax.all_to_all(copies, axis, split_axis=0, concat_axis=0, tiled=True)  7.47 us
    all_to_all x1, waiting for transfers between devices, per_device(): lax.all_to_all(second_scale.astype(jnp.bfloat16), 'node', split_axis=0, c...  5.12 us
    all_to_all x1, starting transfers between devices, per_device(): lax.all_to_all(second_payload, 'node', split_axis=0, concat_axis=0, tiled...  4.35 us
  transfers between devices with their start and end apart: 3, of which 3 were waited for; matrix products, arithmetic and copies ran while one was open for 6% of the time, Pallas kernels for 0%

commit v1 on v0

v1 whole, which is shorter than its diff:
```python
import jax
import jax.numpy as jnp
from jax import lax
from jax.experimental import pallas as pl
from jax.experimental.pallas import tpu as pltpu
from jax.sharding import PartitionSpec as P

BLOCK = 256
MESH = pl.DeviceIdType.MESH
F32 = jnp.float32
BF16 = jnp.bfloat16

NX, NZ, NCORE, NYLO, NYHI = 4, 8, 2, 2, 2
NODES, LOCALS = 32, 8
OWN = 16
TOK = 128
COLS = 512
HALVES = COLS // BLOCK
CHUNKS = 4
SLOTS = NODES // CHUNKS
ROWS = SLOTS * OWN
KEEP = ROWS // NCORE


def quantize_restore(values):
    largest = jnp.max(jnp.abs(values), axis=1, keepdims=True)
    scale = (largest + 1e-06) / 127.0
    payload = (values * (1.0 / scale)).astype(BF16)
    return payload.astype(F32) * scale


def kernel(
    act_hbm, grads_hbm, master_hbm, first_hbm, second_hbm,
    weight_out, first_out, second_out,
    act, at_send, at_recv, g, y_send, y_recv, keep, d_send, d_recv, z_send, z_recv, own_sum,
    master, first, second, new_first, new_second, weight,
    load_sem, g_ss, g_rs, a_ss, a_rs, y_ss, y_rs, d_ss, d_rs, z_ss, z_rs, w_ss, w_rs, store_sem,
):
    node = lax.axis_index("node")
    local = lax.axis_index("local")
    core = node % NCORE
    z = (node // NCORE) % NZ
    y_lo = node // (NCORE * NZ)
    x = local % NX
    y_hi = local // NX

    def node_of(yr, dz, cr):
        return (((y_lo + yr) % NYLO) * NZ + (z + dz) % NZ) * NCORE + (core + cr) % NCORE

    def local_of(hr, dx):
        return ((y_hi + hr) % NYHI) * NX + (x + dx) % NX

    def remote(src, dst, ss, rs, to):
        return pltpu.make_async_remote_copy(
            src_ref=src, dst_ref=dst, send_sem=ss, recv_sem=rs, device_id=to, device_id_type=MESH
        )

    local_peers = [(node, local_of(hr, dx)) for hr in range(NYHI) for dx in range(NX) if hr or dx]
    z_peers = [(node_of(yr, dz, 0), local) for dz in range(NZ) for yr in range(NYLO) if dz or yr]
    partner = (node_of(0, 0, 1), local)
    peers = [*local_peers, *z_peers, partner]

    loads = [
        pltpu.make_async_copy(act_hbm, act, load_sem.at[0]),
        *(
            pltpu.make_async_copy(grads_hbm.at[:, pl.ds(b * BLOCK, BLOCK)], g.at[0, b], load_sem.at[1 + b])
            for b in range(HALVES)
        ),
        pltpu.make_async_copy(master_hbm, master, load_sem.at[1 + HALVES]),
        pltpu.make_async_copy(first_hbm, first, load_sem.at[2 + HALVES]),
        pltpu.make_async_copy(second_hbm, second, load_sem.at[3 + HALVES]),
    ]
    for load in loads:
        load.start()
    barrier = pltpu.get_barrier_semaphore()
    for peer in peers:
        pl.semaphore_signal(barrier, inc=1, device_id=peer, device_id_type=MESH)

    loads[0].wait()

    def transpose_chunk(j, carry):
        for cr in range(NCORE):
            for kk in range(2):
                dz = 4 + j if kk == 0 else 3 - j
                for yr in range(NYLO):
                    slot = j * SLOTS + (cr * 2 + kk) * 2 + yr
                    m = node_of(yr, dz, cr)
                    columns = pl.ds(pl.multiple_of(m * (LOCALS * OWN), LOCALS * OWN), LOCALS * OWN)
                    turned = act[:, columns].T
                    for owner in range(LOCALS):
                        dx = (owner % NX - x + NX) % NX
                        hr = (owner // NX - y_hi + NYHI) % NYHI
                        at_send[dx, hr, slot] = turned[owner * OWN : (owner + 1) * OWN]
        return carry

    lax.fori_loop(0, CHUNKS, transpose_chunk, 0)
    for load in loads[1:]:
        load.wait()
    pl.semaphore_wait(barrier, len(peers))

    def g_copy(dx, b):
        return remote(g.at[0, b], g.at[dx, b], g_ss.at[dx - 1, b], g_rs.at[dx - 1, b], (node, local_of(0, dx)))

    def a_copy(dx, hr, j):
        part = pl.ds(j * SLOTS, SLOTS)
        return remote(
            at_send.at[dx, hr, part], at_recv.at[dx - 1, hr, part],
            a_ss.at[dx - 1, hr, j], a_rs.at[dx - 1, hr, j], (node, local_of(0, dx)),
        )

    def y_copy(j, b):
        return remote(y_send.at[j, b], y_recv.at[j, b], y_ss.at[j, b], y_rs.at[j, b], (node, local_of(1, 0)))

    def d_copy(j, b):
        return remote(d_send.at[j, b], d_recv.at[j, b], d_ss.at[j, b], d_rs.at[j, b], partner)

    def z_copy(j, kk, yr):
        dz = 4 + j if kk == 0 else 3 - j
        return remote(
            z_send.at[j, kk, yr], z_recv.at[j, kk, yr],
            z_ss.at[j, kk, yr], z_rs.at[j, kk, yr], (node_of(yr, dz, 0), local),
        )

    def w_copy(i):
        hr, dx = (i + 1) // NX, (i + 1) % NX
        mine = pl.ds(pl.multiple_of(local * OWN, OWN), OWN)
        return remote(weight, weight_out.at[mine], w_ss.at[i], w_rs.at[i], (node, local_of(hr, dx)))

    across = (1, 3, 2)
    for dx in across:
        g_copy(dx, 0).start()
    for j in range(CHUNKS):
        for dx in across:
            a_copy(dx, 1, j).start()
    for dx in across:
        g_copy(dx, 1).start()
    for j in range(CHUNKS):
        for dx in across:
            a_copy(dx, 0, j).start()

    def ring_sum(hr, j, b):
        part = pl.ds(j * SLOTS, SLOTS)
        total = None
        for dx in range(NX):
            inputs = at_send[0, hr, part] if dx == 0 else at_recv[dx - 1, hr, part]
            grad = jnp.dot(inputs.reshape(ROWS, TOK), g[dx, b], preferred_element_type=F32)
            restored = quantize_restore(grad)
            total = restored if total is None else total + restored
        return total

    for b in range(HALVES):
        for dx in across:
            g_copy(dx, b).wait_recv()

        def partner_rows(j, carry, b=b):
            if b == 0:
                for dx in across:
                    a_copy(dx, 1, j).wait_recv()
            y_send[j, b] = ring_sum(1, j, b).astype(BF16)
            y_copy(j, b).start()
            return carry

        lax.fori_loop(0, CHUNKS, partner_rows, 0)

    def to_owners(j):
        for b in range(HALVES):
            d_copy(j, b).wait_recv()
        for kk in range(2):
            for yr in range(NYLO):
                rows = pl.ds((kk * 2 + yr) * OWN, OWN)
                pair = keep[j, :, rows] + d_recv[j, :, rows]
                for b in range(HALVES):
                    z_send[j, kk, yr, :, b * BLOCK : (b + 1) * BLOCK] = pair[b].astype(BF16)
                    if kk == 1 and yr == 0:
                        own_sum[:, b * BLOCK : (b + 1) * BLOCK] = pair[b]
                if kk == 1 and yr == 0:
                    @pl.when(j < CHUNKS - 1)
                    def _():
                        z_copy(j, kk, yr).start()
                else:
                    z_copy(j, kk, yr).start()

    def own_rows(j, carry):
        for dx in across:
            a_copy(dx, 0, j).wait_recv()
        for b in range(HALVES):
            partial = ring_sum(0, j, b)
            y_copy(j, b).wait_recv()
            restored = quantize_restore(partial + y_recv[j, b].astype(F32))
            keep[j, b] = restored[:KEEP]
            d_send[j, b] = restored[KEEP:]
            d_copy(j, b).start()

        @pl.when(j > 0)
        def _():
            to_owners(j - 1)

        return carry

    lax.fori_loop(0, CHUNKS, own_rows, 0)
    to_owners(CHUNKS - 1)

    total = own_sum[...]
    for j in range(CHUNKS):
        for kk in range(2):
            for yr in range(NYLO):
                if (j, kk, yr) != (CHUNKS - 1, 1, 0):
                    z_copy(j, kk, yr).wait_recv()
                    total = total + z_recv[j, kk, yr].astype(F32)
    grad = total / (NODES * LOCALS)
    first_now = 0.9 * first[...] + 0.1 * grad
    second_now = 0.95 * second[...] + 0.05 * grad * grad
    update = first_now / (1.0 - 0.9**10) / (jnp.sqrt(second_now / (1.0 - 0.95**10)) + 1e-08)
    weight[...] = (master[...] - 0.01 * update).astype(BF16)
    new_first[...] = first_now
    new_second[...] = second_now
    for i in range(LOCALS - 1):
        w_copy(i).start()
    mine = pl.ds(pl.multiple_of(local * OWN, OWN), OWN)
    stores = [
        pltpu.make_async_copy(weight, weight_out.at[mine], store_sem.at[0]),
        pltpu.make_async_copy(new_first, first_out, store_sem.at[1]),
        pltpu.make_async_copy(new_second, second_out, store_sem.at[2]),
    ]
    for store in stores:
        store.start()

    for dx in across:
        for b in range(HALVES):
            g_copy(dx, b).wait_send()

    def drain(j, carry):
        for dx in across:
            for hr in range(NYHI):
                a_copy(dx, hr, j).wait_send()
        for b in range(HALVES):
            y_copy(j, b).wait_send()
            d_copy(j, b).wait_send()
        for kk in range(2):
            for yr in range(NYLO):
                if kk == 1 and yr == 0:
                    @pl.when(j < CHUNKS - 1)
                    def _():
                        z_copy(j, kk, yr).wait_send()
                else:
                    z_copy(j, kk, yr).wait_send()
        return carry

    lax.fori_loop(0, CHUNKS, drain, 0)
    for store in stores:
        store.wait()
    for i in range(LOCALS - 1):
        w_copy(i).wait_recv()
    for i in range(LOCALS - 1):
        w_copy(i).wait_send()


def per_device(activations, out_grads, master, first_moment, second_moment):
    anywhere = pl.BlockSpec(memory_space=pl.ANY)
    dma = pltpu.SemaphoreType.DMA
    vmem = pltpu.VMEM
    return pl.pallas_call(
        kernel,
        out_shape=(
            jax.ShapeDtypeStruct((LOCALS * OWN, COLS), BF16),
            jax.ShapeDtypeStruct((OWN, COLS), F32),
            jax.ShapeDtypeStruct((OWN, COLS), F32),
        ),
        in_specs=[anywhere] * 5,
        out_specs=(anywhere,) * 3,
        scratch_shapes=[
            vmem((TOK, NODES * LOCALS * OWN), BF16),
            vmem((NX, NYHI, NODES, OWN, TOK), BF16),
            vmem((NX - 1, NYHI, NODES, OWN, TOK), BF16),
            vmem((NX, HALVES, TOK, BLOCK), BF16),
            vmem((CHUNKS, HALVES, ROWS, BLOCK), BF16),
            vmem((CHUNKS, HALVES, ROWS, BLOCK), BF16),
            vmem((CHUNKS, HALVES, KEEP, BLOCK), F32),
            vmem((CHUNKS, HALVES, KEEP, BLOCK), F32),
            vmem((CHUNKS, HALVES, KEEP, BLOCK), F32),
            vmem((CHUNKS, 2, NYLO, OWN, COLS), BF16),
            vmem((CHUNKS, 2, NYLO, OWN, COLS), BF16),
            vmem((OWN, COLS), F32),
            vmem((OWN, COLS), F32),
            vmem((OWN, COLS), F32),
            vmem((OWN, COLS), F32),
            vmem((OWN, COLS), F32),
            vmem((OWN, COLS), F32),
            vmem((OWN, COLS), BF16),
            dma((4 + HALVES,)),
            dma((NX - 1, HALVES)),
            dma((NX - 1, HALVES)),
            dma((NX - 1, NYHI, CHUNKS)),
            dma((NX - 1, NYHI, CHUNKS)),
            dma((CHUNKS, HALVES)),
            dma((CHUNKS, HALVES)),
            dma((CHUNKS, HALVES)),
            dma((CHUNKS, HALVES)),
            dma((CHUNKS, 2, NYLO)),
            dma((CHUNKS, 2, NYLO)),
            dma((LOCALS - 1,)),
            dma((LOCALS - 1,)),
            dma((3,)),
        ],
        compiler_params=pltpu.CompilerParams(collective_id=0, has_side_effects=True),
    )(activations, out_grads, master, first_moment, second_moment)


def solution(mesh):
    rows = P(("node", "local"), None)
    return jax.shard_map(
        per_device,
        mesh=mesh,
        in_specs=(rows,) * 5,
        out_specs=(P("node", None), rows, rows),
        check_vma=False,
    )
```

time: 107 us -> 50.5 us (0.47); the launches traced: 105 us -> 50.3 us
  Pallas kernels: 0 us -> 46.7 us
  waiting for transfers between devices: 35.6 us -> 0 us
  blocking collectives: 28.6 us -> 0 us
  starting transfers between devices: 22.4 us -> 0 us
  local copies, waits for them, and re-layouts: 12.4 us -> 2.96 us
  other arithmetic: 3.73 us -> 0 us
  matrix products: 1.3 us -> 0 us
    pallas_call x0 -> x1, Pallas kernels: none -> 46.7 us  [per_device(): pl.pallas_call(kernel, out_shape=(jax.ShapeDtypeStruct((LOCALS * OWN, COL...]
    all_to_all x3 -> x0, waiting for transfers between devices: 35.6 us -> none  [the longest x1 15.6 us: from_everyone(): return lax.all_to_all(copies, axis, split_axis=0, concat_axis=0, tiled=True)]
    all_to_all x2 -> x0, blocking collectives: 28.6 us -> none  [the longest x1 18.8 us: per_device(): lax.all_to_all(bands, 'local', split_axis=2, concat_axis=0, tiled=True)]
    all_to_all x3 -> x0, starting transfers between devices: 22.4 us -> none  [the longest x1 10.6 us: per_device(): lax.all_to_all(second_scale.astype(jnp.bfloat16), 'node', split_axis=0, c...]
    abs x2 -> x0, local copies, waits for them, and re-layouts: 3.21 us -> none  [quantize(): largest = jnp.max(jnp.abs(blocks), axis=-1)]
    div x3 -> x0, local copies, waits for them, and re-layouts: 1.64 us -> none  [the longest x2 1.45 us: quantize(): payload = (blocks / scale[..., None]).astype(jnp.bfloat16)]
    convert_element_type x2 -> x0, other arithmetic: 1.63 us -> none  [the longest x1 0.99 us: quantize(): payload = (blocks / scale[..., None]).astype(jnp.bfloat16)]
    mul x2 -> x0, local copies, waits for them, and re-layouts: 1.44 us -> none  [restore_sum(): values = blocks.astype(jnp.float32) * scale[..., None]]
  transfers between devices with their start and end apart: 3 -> 0, of which waited for: 3 -> 0; matrix products, arithmetic and copies ran while one was open for 6% -> 0% of each run, Pallas kernels for 0% -> 0%
where the time goes in v1:
time: 50.5 us; the launch traced here: 50.3 us
  Pallas kernels  46.7 us (92%)
  local copies, waits for them, and re-layouts  2.96 us (6%)
  between operations  0.65 us (1%)
    pallas_call x1, Pallas kernels, per_device(): pl.pallas_call(kernel, out_shape=(jax.ShapeDtypeStruct((LOCALS * OWN, COL...  46.7 us
    unnamed x7, local copies, waits for them, and re-layouts  2.96 us

profile of v1, /device:TPU:1, one launch (start us, length us, event | category | flops | bytes accessed | tf_op | source)
XLA Modules:
  0.0 50.3 jit_solution(7390598849790476625)
XLA Ops:
  0.6 46.7 %shard_map.76 = (bf16[128,512]{1,0:T(8,128)(2,1)}, f32[16,512]{1,0:T(8,128)}, f32[16,512]{1,0:T(8,128)}) custom-call(bf16[128,4096]{1,0:T(8,128)(2,1)} %act_hbm.1, bf16[128,512]{1,0:T(8,128)(2,1)} %grads_hbm.1, f32[16,512]{1,0:T(8,128)} %master_hbm.1, f32[16,512]{1,0:T(8,128)} %first_hbm.1, f32[16,512]{1,0:T(8,128)} %second_hbm.1), custom_call_target="tpu_custom_call" | custom-call | tf_op jit(solution)/shard_map/pallas_call | solution.py:262
  47.3 0.0 copy-start.1
  47.3 1.6 %copy.11 = bf16[128,512]{1,0:T(8,128)(2,1)} copy(bf16[128,512]{1,0:T(8,128)(2,1)} %get-tuple-element.6) | data formatting | bytes 262144
  48.9 0.0 copy-done.1
  48.9 0.0 copy-start
  48.9 0.6 %copy.12 = f32[16,512]{1,0:T(8,128)} copy(f32[16,512]{1,0:T(8,128)S(1)} %copy-done.1) | data formatting | bytes 65536
  49.5 0.2 copy-done
  49.6 0.6 %copy.13 = f32[16,512]{1,0:T(8,128)} copy(f32[16,512]{1,0:T(8,128)S(1)} %copy-done) | data formatting | bytes 65536
Async XLA Ops:
  47.3 1.6 %copy-start.1 = (f32[16,512]{1,0:T(8,128)S(1)}, f32[16,512]{1,0:T(8,128)}, u32[]{:S(2)}) copy-start(f32[16,512]{1,0:T(8,128)} %get-tuple-element.7) | copy-start | bytes 98308
  48.9 0.8 %copy-start = (f32[16,512]{1,0:T(8,128)S(1)}, f32[16,512]{1,0:T(8,128)}, u32[]{:S(2)}) copy-start(f32[16,512]{1,0:T(8,128)} %get-tuple-element.8) | copy-start | bytes 98308

commit v2 on v1

v2 whole, which is shorter than its diff:
```python
import jax
import jax.numpy as jnp
from jax import lax
from jax.experimental import pallas as pl
from jax.experimental.pallas import tpu as pltpu
from jax.sharding import PartitionSpec as P

BLOCK = 256
MESH = pl.DeviceIdType.MESH
F32 = jnp.float32
BF16 = jnp.bfloat16

NX, NY, NZ, NCORE, NYLO, NYHI = 4, 4, 8, 2, 2, 2
NODES, LOCALS = 32, 8
OWN = 16
TOK = 128
COLS = 512
HALVES = COLS // BLOCK
UNITS = 2
FAR = ((4, 3, 5, 2), (6, 1, 7, 0))
QUADS = 4
CLASSES = 4
STEP = (2, 1, 3, 0)
OWN_CLASS = 3
SLOTS = NCORE * QUADS
ROWS = SLOTS * OWN
KEEP = ROWS // NCORE


def quantize_restore(values):
    largest = jnp.max(jnp.abs(values), axis=1, keepdims=True)
    scale = (largest + 1e-06) / 127.0
    payload = (values * (1.0 / scale)).astype(BF16)
    return payload.astype(F32) * scale


def kernel(
    act_hbm, grads_hbm, master_hbm, first_hbm, second_hbm,
    weight_out, first_out, second_out,
    act, at_send, at_recv, g, base, y_send, y_recv, keep, d_send, d_recv, z_send, z_recv, own_sum,
    master, first, second, new_first, new_second, weight,
    load_sem, g_ss, g_rs, a_ss, a_rs, y_ss, y_rs, d_ss, d_rs, z_ss, z_rs, w_ss, w_rs, store_sem,
):
    node = lax.axis_index("node")
    local = lax.axis_index("local")
    core = node % NCORE
    z = (node // NCORE) % NZ
    x = local % NX
    y_hi = local // NX
    y = y_hi * NYLO + node // (NCORE * NZ)

    def device(dx, dy, dz, dc):
        to_y = (y + dy) % NY
        to_node = ((to_y % NYLO) * NZ + (z + dz) % NZ) * NCORE + (core + dc) % NCORE
        return to_node, (to_y // NYLO) * NX + (x + dx) % NX

    def remote(src, dst, ss, rs, to):
        return pltpu.make_async_remote_copy(
            src_ref=src, dst_ref=dst, send_sem=ss, recv_sem=rs, device_id=to, device_id_type=MESH
        )

    peers = [
        *(device(dx, dy, 0, 0) for dy in (0, 2) for dx in range(NX) if dx or dy),
        *(device(0, dy, 0, 0) for dy in (1, 3)),
        *(device(0, 0, dz, 0) for dz in range(1, NZ)),
        device(0, 0, 0, 1),
    ]

    loads = [
        pltpu.make_async_copy(act_hbm, act, load_sem.at[0]),
        *(
            pltpu.make_async_copy(grads_hbm.at[:, pl.ds(b * BLOCK, BLOCK)], g.at[0, b], load_sem.at[1 + b])
            for b in range(HALVES)
        ),
        pltpu.make_async_copy(master_hbm, master, load_sem.at[1 + HALVES]),
        pltpu.make_async_copy(first_hbm, first, load_sem.at[2 + HALVES]),
        pltpu.make_async_copy(second_hbm, second, load_sem.at[3 + HALVES]),
    ]
    for load in loads:
        load.start()
    barrier = pltpu.get_barrier_semaphore()
    for peer in peers:
        pl.semaphore_signal(barrier, inc=1, device_id=peer, device_id_type=MESH)

    loads[0].wait()
    next_hi = ((y + 1) % NY) // NYLO

    def transpose_pair(i, carry):
        yr, cr = i // NCORE, i % NCORE
        for u in range(UNITS):
            for q in range(QUADS):
                m = device(0, yr, FAR[u][q], cr)[0]
                columns = pl.ds(pl.multiple_of(m * (LOCALS * OWN), LOCALS * OWN), LOCALS * OWN)
                turned = act[:, columns].T
                for owner in range(LOCALS):
                    dx = (owner % NX - x + NX) % NX
                    hi = owner // NX
                    kind = (1 - yr) * OWN_CLASS * ((hi + y_hi + 1) % NYHI) + yr * (1 + (hi + next_hi) % NYHI)
                    at_send[dx, kind, u, cr * QUADS + q] = turned[owner * OWN : (owner + 1) * OWN]
        return carry

    lax.fori_loop(0, NYLO * NCORE, transpose_pair, 0)
    for load in loads[1:]:
        load.wait()

    def ring_term(dx, kind, u, b):
        inputs = at_send[0, kind, u] if dx == 0 else at_recv[dx - 1, kind, u]
        grad = jnp.dot(inputs.reshape(ROWS, TOK), g[dx, b], preferred_element_type=F32)
        return quantize_restore(grad)

    def own_terms(kind, carry):
        for u in range(UNITS):
            for b in range(HALVES):
                base[kind, u, b] = ring_term(0, kind, u, b)
        return carry

    lax.fori_loop(0, CLASSES, own_terms, 0)
    pl.semaphore_wait(barrier, len(peers))

    def g_copy(dx, b):
        return remote(g.at[0, b], g.at[dx, b], g_ss.at[dx - 1, b], g_rs.at[dx - 1, b], device(dx, 0, 0, 0))

    def a_copy(dx, kind, u):
        return remote(
            at_send.at[dx, kind, u], at_recv.at[dx - 1, kind, u],
            a_ss.at[dx - 1, kind, u], a_rs.at[dx - 1, kind, u], device(dx, 0, 0, 0),
        )

    def y_copy(kind, step, u, b):
        return remote(
            y_send.at[kind, u, b], y_recv.at[kind, u, b],
            y_ss.at[kind, u, b], y_rs.at[kind, u, b], device(0, step, 0, 0),
        )

    def d_copy(u, b):
        return remote(d_send.at[u, b], d_recv.at[u, b], d_ss.at[u, b], d_rs.at[u, b], device(0, 0, 0, 1))

    def z_copy(u, q):
        return remote(z_send.at[u, q], z_recv.at[u, q], z_ss.at[u, q], z_rs.at[u, q], device(0, 0, FAR[u][q], 0))

    def w_copy(i):
        dy, dx = 2 * ((i + 1) // NX), (i + 1) % NX
        mine = pl.ds(pl.multiple_of(local * OWN, OWN), OWN)
        return remote(weight, weight_out.at[mine], w_ss.at[i], w_rs.at[i], device(dx, dy, 0, 0))

    across = (1, 3, 2)

    def send_inputs(kind, u):
        for dx in across:
            a_copy(dx, kind, u).start()

    for dx in across:
        g_copy(dx, 0).start()
    for u in range(UNITS):
        send_inputs(0, u)
    for dx in across:
        g_copy(dx, 1).start()
    for u in range(UNITS):
        for kind in (1, 2):
            send_inputs(kind, u)
    for u in range(UNITS):
        send_inputs(OWN_CLASS, u)

    def ring_sum(kind, u, b):
        total = base[kind, u, b]
        for dx in range(1, NX):
            total = total + ring_term(dx, kind, u, b)
        return total

    for b in range(HALVES):
        for dx in across:
            g_copy(dx, b).wait_recv()
        for u in range(UNITS):
            if b == 0:
                for dx in across:
                    a_copy(dx, 0, u).wait_recv()
            y_send[0, u, b] = ring_sum(0, u, b).astype(BF16)
            y_copy(0, STEP[0], u, b).start()

    def next_rows(i, carry):
        kind, u = 1 + i % 2, i // 2
        for dx in across:
            a_copy(dx, kind, u).wait_recv()
        for b in range(HALVES):
            y_send[kind, u, b] = ring_sum(kind, u, b).astype(BF16)
            y_copy(kind, 2 * kind - 1, u, b).start()
        return carry

    lax.fori_loop(0, 2 * UNITS, next_rows, 0)

    def own_node(u):
        for dx in across:
            a_copy(dx, OWN_CLASS, u).wait_recv()
        for b in range(HALVES):
            y_copy(0, STEP[0], u, b).wait_recv()
            base[OWN_CLASS, u, b] = quantize_restore(ring_sum(OWN_CLASS, u, b) + y_recv[0, u, b].astype(F32))

    def next_node(u):
        for b in range(HALVES):
            for kind in (1, 2):
                y_copy(kind, STEP[kind], u, b).wait_recv()
            both = quantize_restore(y_recv[1, u, b].astype(F32) + y_recv[2, u, b].astype(F32))
            both = both + base[OWN_CLASS, u, b]
            keep[u, b] = both[:KEEP]
            d_send[u, b] = both[KEEP:]
            d_copy(u, b).start()

    def to_owners(u):
        for b in range(HALVES):
            d_copy(u, b).wait_recv()
        for q in range(QUADS):
            rows = pl.ds(q * OWN, OWN)
            pair = keep[u, :, rows] + d_recv[u, :, rows]
            for b in range(HALVES):
                if FAR[u][q] == 0:
                    own_sum[:, b * BLOCK : (b + 1) * BLOCK] = pair[b]
                else:
                    z_send[u, q, :, b * BLOCK : (b + 1) * BLOCK] = pair[b].astype(BF16)
            if FAR[u][q]:
                z_copy(u, q).start()

    own_node(0)
    next_node(0)
    own_node(1)
    to_owners(0)
    next_node(1)
    to_owners(1)

    total = own_sum[...]
    for u in range(UNITS):
        for q in range(QUADS):
            if FAR[u][q]:
                z_copy(u, q).wait_recv()
                total = total + z_recv[u, q].astype(F32)
    grad = total / (NODES * LOCALS)
    first_now = 0.9 * first[...] + 0.1 * grad
    second_now = 0.95 * second[...] + 0.05 * grad * grad
    update = first_now / (1.0 - 0.9**10) / (jnp.sqrt(second_now / (1.0 - 0.95**10)) + 1e-08)
    weight[...] = (master[...] - 0.01 * update).astype(BF16)
    new_first[...] = first_now
    new_second[...] = second_now
    for i in reversed(range(LOCALS - 1)):
        w_copy(i).start()
    mine = pl.ds(pl.multiple_of(local * OWN, OWN), OWN)
    stores = [
        pltpu.make_async_copy(weight, weight_out.at[mine], store_sem.at[0]),
        pltpu.make_async_copy(new_first, first_out, store_sem.at[1]),
        pltpu.make_async_copy(new_second, second_out, store_sem.at[2]),
    ]
    for store in stores:
        store.start()

    for dx in across:
        for b in range(HALVES):
            g_copy(dx, b).wait_send()

    def drain(u, carry):
        for kind in range(CLASSES):
            for dx in across:
                a_copy(dx, kind, u).wait_send()
        for b in range(HALVES):
            for kind in range(OWN_CLASS):
                y_copy(kind, STEP[kind], u, b).wait_send()
            d_copy(u, b).wait_send()
        return carry

    lax.fori_loop(0, UNITS, drain, 0)
    for u in range(UNITS):
        for q in range(QUADS):
            if FAR[u][q]:
                z_copy(u, q).wait_send()
    for store in stores:
        store.wait()
    for i in range(LOCALS - 1):
        w_copy(i).wait_send()
    for i in range(LOCALS - 1):
        w_copy(i).wait_recv()


def per_device(activations, out_grads, master, first_moment, second_moment):
    anywhere = pl.BlockSpec(memory_space=pl.ANY)
    dma = pltpu.SemaphoreType.DMA
    vmem = pltpu.VMEM
    return pl.pallas_call(
        kernel,
        out_shape=(
            jax.ShapeDtypeStruct((LOCALS * OWN, COLS), BF16),
            jax.ShapeDtypeStruct((OWN, COLS), F32),
            jax.ShapeDtypeStruct((OWN, COLS), F32),
        ),
        in_specs=[anywhere] * 5,
        out_specs=(anywhere,) * 3,
        scratch_shapes=[
            vmem((TOK, NODES * LOCALS * OWN), BF16),
            vmem((NX, CLASSES, UNITS, SLOTS, OWN, TOK), BF16),
            vmem((NX - 1, CLASSES, UNITS, SLOTS, OWN, TOK), BF16),
            vmem((NX, HALVES, TOK, BLOCK), BF16),
            vmem((CLASSES, UNITS, HALVES, ROWS, BLOCK), F32),
            vmem((CLASSES - 1, UNITS, HALVES, ROWS, BLOCK), BF16),
            vmem((CLASSES - 1, UNITS, HALVES, ROWS, BLOCK), BF16),
            vmem((UNITS, HALVES, KEEP, BLOCK), F32),
            vmem((UNITS, HALVES, KEEP, BLOCK), F32),
            vmem((UNITS, HALVES, KEEP, BLOCK), F32),
            vmem((UNITS, QUADS, OWN, COLS), BF16),
            vmem((UNITS, QUADS, OWN, COLS), BF16),
            vmem((OWN, COLS), F32),
            vmem((OWN, COLS), F32),
            vmem((OWN, COLS), F32),
            vmem((OWN, COLS), F32),
            vmem((OWN, COLS), F32),
            vmem((OWN, COLS), F32),
            vmem((OWN, COLS), BF16),
            dma((4 + HALVES,)),
            dma((NX - 1, HALVES)),
            dma((NX - 1, HALVES)),
            dma((NX - 1, CLASSES, UNITS)),
            dma((NX - 1, CLASSES, UNITS)),
            dma((CLASSES - 1, UNITS, HALVES)),
            dma((CLASSES - 1, UNITS, HALVES)),
            dma((UNITS, HALVES)),
            dma((UNITS, HALVES)),
            dma((UNITS, QUADS)),
            dma((UNITS, QUADS)),
            dma((LOCALS - 1,)),
            dma((LOCALS - 1,)),
            dma((3,)),
        ],
        compiler_params=pltpu.CompilerParams(collective_id=0, has_side_effects=True),
    )(activations, out_grads, master, first_moment, second_moment)


def solution(mesh):
    rows = P(("node", "local"), None)
    return jax.shard_map(
        per_device,
        mesh=mesh,
        in_specs=(rows,) * 5,
        out_specs=(P("node", None), rows, rows),
        check_vma=False,
    )
```

time: 50.5 us -> 46.7 us (0.925)
  Pallas kernels: 46.7 us -> 42.9 us
    pallas_call x1, Pallas kernels: 46.7 us -> 42.9 us  [per_device(): pl.pallas_call(kernel, out_shape=(jax.ShapeDtypeStruct((LOCALS * OWN, COL...]
where the time goes in v2:
time: 46.7 us; the launch traced here: 46.5 us
  Pallas kernels  42.9 us (92%)
  local copies, waits for them, and re-layouts  2.96 us (6%)
  between operations  0.65 us (1%)
    pallas_call x1, Pallas kernels, per_device(): pl.pallas_call(kernel, out_shape=(jax.ShapeDtypeStruct((LOCALS * OWN, COL...  42.9 us
    unnamed x7, local copies, waits for them, and re-layouts  2.96 us

profile of v2, /device:TPU:1, one launch (start us, length us, event | category | flops | bytes accessed | tf_op | source)
XLA Modules:
  0.0 46.5 jit_solution(10009948935346886183)
XLA Ops:
  0.6 42.9 %shard_map.76 = (bf16[128,512]{1,0:T(8,128)(2,1)}, f32[16,512]{1,0:T(8,128)}, f32[16,512]{1,0:T(8,128)}) custom-call(bf16[128,4096]{1,0:T(8,128)(2,1)} %act_hbm.1, bf16[128,512]{1,0:T(8,128)(2,1)} %grads_hbm.1, f32[16,512]{1,0:T(8,128)} %master_hbm.1, f32[16,512]{1,0:T(8,128)} %first_hbm.1, f32[16,512]{1,0:T(8,128)} %second_hbm.1), custom_call_target="tpu_custom_call" | custom-call | tf_op jit(solution)/shard_map/pallas_call | solution.py:284
  43.6 0.0 copy-start.1
  43.6 1.6 %copy.11 = bf16[128,512]{1,0:T(8,128)(2,1)} copy(bf16[128,512]{1,0:T(8,128)(2,1)} %get-tuple-element.6) | data formatting | bytes 262144
  45.1 0.0 copy-done.1
  45.1 0.0 copy-start
  45.1 0.6 %copy.12 = f32[16,512]{1,0:T(8,128)} copy(f32[16,512]{1,0:T(8,128)S(1)} %copy-done.1) | data formatting | bytes 65536
  45.8 0.2 copy-done
  45.9 0.6 %copy.13 = f32[16,512]{1,0:T(8,128)} copy(f32[16,512]{1,0:T(8,128)S(1)} %copy-done) | data formatting | bytes 65536
Async XLA Ops:
  43.6 1.6 %copy-start.1 = (f32[16,512]{1,0:T(8,128)S(1)}, f32[16,512]{1,0:T(8,128)}, u32[]{:S(2)}) copy-start(f32[16,512]{1,0:T(8,128)} %get-tuple-element.7) | copy-start | bytes 98308
  45.1 0.8 %copy-start = (f32[16,512]{1,0:T(8,128)S(1)}, f32[16,512]{1,0:T(8,128)}, u32[]{:S(2)}) copy-start(f32[16,512]{1,0:T(8,128)} %get-tuple-element.8) | copy-start | bytes 98308

commit v3 on v2

--- a/solution.py
+++ b/solution.py
@@ -38,8 +38,8 @@
     act_hbm, grads_hbm, master_hbm, first_hbm, second_hbm,
     weight_out, first_out, second_out,
     act, at_send, at_recv, g, base, y_send, y_recv, keep, d_send, d_recv, z_send, z_recv, own_sum,
-    master, first, second, new_first, new_second, weight,
-    load_sem, g_ss, g_rs, a_ss, a_rs, y_ss, y_rs, d_ss, d_rs, z_ss, z_rs, w_ss, w_rs, store_sem,
+    master, first, second, weight,
+    load_sem, g_ss, g_rs, a_ss, a_rs, y_ss, y_rs, d_ss, d_rs, z_ss, z_rs, w_ss, w_rs,
 ):
     node = lax.axis_index("node")
     local = lax.axis_index("local")
@@ -108,6 +108,52 @@
         grad = jnp.dot(inputs.reshape(ROWS, TOK), g[dx, b], preferred_element_type=F32)
         return quantize_restore(grad)
 
+    pl.semaphore_wait(barrier, len(peers))
+
+    def g_copy(dx, b):
+        return remote(g.at[0, b], g.at[dx, b], g_ss.at[dx - 1, b], g_rs.at[dx - 1, b], device(dx, 0, 0, 0))
+
+    def a_copy(dx, kind, u):
+        return remote(
+            at_send.at[dx, kind, u], at_recv.at[dx - 1, kind, u],
+            a_ss.at[dx - 1, kind, u], a_rs.at[dx - 1, kind, u], device(dx, 0, 0, 0),
+        )
+
+    def y_copy(kind, step, u, b):
+        return remote(
+            y_send.at[kind, u, b], y_recv.at[kind, u, b],
+            y_ss.at[kind, u, b], y_rs.at[kind, u, b], device(0, step, 0, 0),
+        )
+
+    def d_copy(u, b):
+        return remote(d_send.at[u, b], d_recv.at[u, b], d_ss.at[u, b], d_rs.at[u, b], device(0, 0, 0, 1))
+
+    def z_copy(u, q):
+        return remote(z_send.at[u, q], z_recv.at[u, q], z_ss.at[u, q], z_rs.at[u, q], device(0, 0, FAR[u][q], 0))
+
+    def w_copy(i):
+        dy, dx = 2 * ((i + 1) // NX), (i + 1) % NX
+        mine = pl.ds(pl.multiple_of(local * OWN, OWN), OWN)
+        return remote(weight, weight_out.at[mine], w_ss.at[i], w_rs.at[i], device(dx, dy, 0, 0))
+
+    across = (1, 3, 2)
+
+    def send_inputs(kind, u):
+        for dx in across:
+            a_copy(dx, kind, u).start()
+
+    for dx in across:
+        g_copy(dx, 0).start()
+    for u in range(UNITS):
+        send_inputs(0, u)
+    for dx in across:
+        g_copy(dx, 1).start()
+    for u in range(UNITS):
+        for kind in (1, 2):
+            send_inputs(kind, u)
+    for u in range(UNITS):
+        send_inputs(OWN_CLASS, u)
+
     def own_terms(kind, carry):
         for u in range(UNITS):
             for b in range(HALVES):
@@ -115,51 +161,6 @@
         return carry
 
     lax.fori_loop(0, CLASSES, own_terms, 0)
-    pl.semaphore_wait(barrier, len(peers))
-
-    def g_copy(dx, b):
-        return remote(g.at[0, b], g.at[dx, b], g_ss.at[dx - 1, b], g_rs.at[dx - 1, b], device(dx, 0, 0, 0))
-
-    def a_copy(dx, kind, u):
-        return remote(
-            at_send.at[dx, kind, u], at_recv.at[dx - 1, kind, u],
-            a_ss.at[dx - 1, kind, u], a_rs.at[dx - 1, kind, u], device(dx, 0, 0, 0),
-        )
-
-    def y_copy(kind, step, u, b):
-        return remote(
-            y_send.at[kind, u, b], y_recv.at[kind, u, b],
-            y_ss.at[kind, u, b], y_rs.at[kind, u, b], device(0, step, 0, 0),
-        )
-
-    def d_copy(u, b):
-        return remote(d_send.at[u, b], d_recv.at[u, b], d_ss.at[u, b], d_rs.at[u, b], device(0, 0, 0, 1))
-
-    def z_copy(u, q):
-        return remote(z_send.at[u, q], z_recv.at[u, q], z_ss.at[u, q], z_rs.at[u, q], device(0, 0, FAR[u][q], 0))
-
-    def w_copy(i):
-        dy, dx = 2 * ((i + 1) // NX), (i + 1) % NX
-        mine = pl.ds(pl.multiple_of(local * OWN, OWN), OWN)
-        return remote(weight, weight_out.at[mine], w_ss.at[i], w_rs.at[i], device(dx, dy, 0, 0))
-
-    across = (1, 3, 2)
-
-    def send_inputs(kind, u):
-        for dx in across:
-            a_copy(dx, kind, u).start()
-
-    for dx in across:
-        g_copy(dx, 0).start()
-    for u in range(UNITS):
-        send_inputs(0, u)
-    for dx in across:
-        g_copy(dx, 1).start()
-    for u in range(UNITS):
-        for kind in (1, 2):
-            send_inputs(kind, u)
-    for u in range(UNITS):
-        send_inputs(OWN_CLASS, u)
 
     def ring_sum(kind, u, b):
         total = base[kind, u, b]
@@ -237,18 +238,11 @@
     second_now = 0.95 * second[...] + 0.05 * grad * grad
     update = first_now / (1.0 - 0.9**10) / (jnp.sqrt(second_now / (1.0 - 0.95**10)) + 1e-08)
     weight[...] = (master[...] - 0.01 * update).astype(BF16)
-    new_first[...] = first_now
-    new_second[...] = second_now
     for i in reversed(range(LOCALS - 1)):
         w_copy(i).start()
-    mine = pl.ds(pl.multiple_of(local * OWN, OWN), OWN)
-    stores = [
-        pltpu.make_async_copy(weight, weight_out.at[mine], store_sem.at[0]),
-        pltpu.make_async_copy(new_first, first_out, store_sem.at[1]),
-        pltpu.make_async_copy(new_second, second_out, store_sem.at[2]),
-    ]
-    for store in stores:
-        store.start()
+    weight_out[pl.ds(pl.multiple_of(local * OWN, OWN), OWN)] = weight[...]
+    first_out[...] = first_now
+    second_out[...] = second_now
 
     for dx in across:
         for b in range(HALVES):
@@ -269,27 +263,39 @@
         for q in range(QUADS):
             if FAR[u][q]:
                 z_copy(u, q).wait_send()
-    for store in stores:
-        store.wait()
     for i in range(LOCALS - 1):
         w_copy(i).wait_send()
     for i in range(LOCALS - 1):
         w_copy(i).wait_recv()
 
 
+def hand_out(weight, first, second, weight_out, first_out, second_out, sem):
+    copies = [
+        pltpu.make_async_copy(weight, weight_out, sem.at[0]),
+        pltpu.make_async_copy(first, first_out, sem.at[1]),
+        pltpu.make_async_copy(second, second_out, sem.at[2]),
+    ]
+    for copy in copies:
+        copy.start()
+    for copy in copies:
+        copy.wait()
+
+
 def per_device(activations, out_grads, master, first_moment, second_moment):
     anywhere = pl.BlockSpec(memory_space=pl.ANY)
     dma = pltpu.SemaphoreType.DMA
     vmem = pltpu.VMEM
-    return pl.pallas_call(
+    results = (
+        jax.ShapeDtypeStruct((LOCALS * OWN, COLS), BF16),
+        jax.ShapeDtypeStruct((OWN, COLS), F32),
+        jax.ShapeDtypeStruct((OWN, COLS), F32),
+    )
+    arguments = (activations, out_grads, master, first_moment, second_moment)
+    made = pl.pallas_call(
         kernel,
-        out_shape=(
-            jax.ShapeDtypeStruct((LOCALS * OWN, COLS), BF16),
-            jax.ShapeDtypeStruct((OWN, COLS), F32),
-            jax.ShapeDtypeStruct((OWN, COLS), F32),
-        ),
-        in_specs=[anywhere] * 5,
-        out_specs=(anywhere,) * 3,
+        out_shape=tuple(vmem(result.shape, result.dtype) for result in results),
+        in_specs=[pl.BlockSpec(memory_space=pltpu.HBM)] * 5,
+        out_specs=(pl.BlockSpec(memory_space=vmem),) * 3,
         scratch_shapes=[
             vmem((TOK, NODES * LOCALS * OWN), BF16),
             vmem((NX, CLASSES, UNITS, SLOTS, OWN, TOK), BF16),
@@ -303,8 +309,6 @@
             vmem((UNITS, HALVES, KEEP, BLOCK), F32),
             vmem((UNITS, QUADS, OWN, COLS), BF16),
             vmem((UNITS, QUADS, OWN, COLS), BF16),
-            vmem((OWN, COLS), F32),
-            vmem((OWN, COLS), F32),
             vmem((OWN, COLS), F32),
             vmem((OWN, COLS), F32),
             vmem((OWN, COLS), F32),
@@ -323,10 +327,19 @@
             dma((UNITS, QUADS)),
             dma((LOCALS - 1,)),
             dma((LOCALS - 1,)),
-            dma((3,)),
         ],
-        compiler_params=pltpu.CompilerParams(collective_id=0, has_side_effects=True),
-    )(activations, out_grads, master, first_moment, second_moment)
+        compiler_params=pltpu.CompilerParams(
+            collective_id=0, has_side_effects=True, vmem_limit_bytes=16 * 1024 * 1024
+        ),
+    )(*(pltpu.with_memory_space_constraint(argument, pltpu.HBM) for argument in arguments))
+    return pl.pallas_call(
+        hand_out,
+        out_shape=results,
+        in_specs=[pl.BlockSpec(memory_space=vmem)] * 3,
+        out_specs=(anywhere,) * 3,
+        scratch_shapes=[dma((3,))],
+        compiler_params=pltpu.CompilerParams(vmem_limit_bytes=1024 * 1024),
+    )(*made)
 
 
 def solution(mesh):

time: 46.7 us -> 44.3 us (0.949)
  local copies, waits for them, and re-layouts: 2.96 us -> 0 us
  Pallas kernels: 42.9 us -> 43.4 us
    unnamed x7 -> x0, local copies, waits for them, and re-layouts: 2.96 us -> none
    pallas_call x1 -> x2, Pallas kernels: 42.9 us -> 43.4 us  [the longest x1 42.7 us: per_device(): pl.pallas_call(kernel, out_shape=tuple((vmem(result.shape, result.dtype)...]
where the time goes in v3:
time: 44.3 us; the launch traced here: 44 us
  Pallas kernels  43.4 us (98%)
  between operations  0.64 us (1%)
    pallas_call x1, Pallas kernels, per_device(): pl.pallas_call(kernel, out_shape=tuple((vmem(result.shape, result.dtype)...  42.7 us

profile of v3, /device:TPU:1, one launch (start us, length us, event | category | flops | bytes accessed | tf_op | source)
XLA Modules:
  0.0 44.0 jit_solution(7753066966517541099)
XLA Ops:
  0.6 42.7 %shard_map.76 = (bf16[128,512]{1,0:T(8,128)(2,1)S(1)}, f32[16,512]{1,0:T(8,128)S(1)}, f32[16,512]{1,0:T(8,128)S(1)}) custom-call(bf16[128,4096]{1,0:T(8,128)(2,1)} %act_hbm.1, bf16[128,512]{1,0:T(8,128)(2,1)} %grads_hbm.1, f32[16,512]{1,0:T(8,128)} %master_hbm.1, f32[16,512]{1,0:T(8,128)} %first_hbm.1, f32[16,512]{1,0:T(8,128)} %second_hbm.1), custom_call_target="tpu_custom_call" | custom-call | tf_op jit(solution)/shard_map/pallas_call | solution.py:294
  43.3 0.7 %shard_map.77 = (bf16[128,512]{1,0:T(8,128)(2,1)}, f32[16,512]{1,0:T(8,128)}, f32[16,512]{1,0:T(8,128)}) custom-call(bf16[128,512]{1,0:T(8,128)(2,1)S(1)} %get-tuple-element.6.weight, f32[16,512]{1,0:T(8,128)S(1)} %get-tuple-element.7.first, f32[16,512]{1,0:T(8,128)S(1)} %get-tuple-element.8.second), custom_call_target="tpu_custom_call" | custom-call | tf_op jit(solution)/shard_map/pallas_call | solution.py:335

commit v4 on v3

--- a/solution.py
+++ b/solution.py
@@ -25,6 +25,7 @@
 SLOTS = NCORE * QUADS
 ROWS = SLOTS * OWN
 KEEP = ROWS // NCORE
+HOPS = NZ // 2 - 1
 
 
 def quantize_restore(values):
@@ -39,7 +40,7 @@
     weight_out, first_out, second_out,
     act, at_send, at_recv, g, base, y_send, y_recv, keep, d_send, d_recv, z_send, z_recv, own_sum,
     master, first, second, weight,
-    load_sem, g_ss, g_rs, a_ss, a_rs, y_ss, y_rs, d_ss, d_rs, z_ss, z_rs, w_ss, w_rs,
+    load_sem, g_ss, g_rs, a_ss, a_rs, y_ss, y_rs, d_ss, d_rs, z_ss, z_rs, w_ss, w_rs, hop_sem,
 ):
     node = lax.axis_index("node")
     local = lax.axis_index("local")
@@ -59,12 +60,20 @@
             src_ref=src, dst_ref=dst, send_sem=ss, recv_sem=rs, device_id=to, device_id_type=MESH
         )
 
+    beside = [device(0, 0, 1, 0), device(0, 0, NZ - 1, 0)]
     peers = [
-        *(device(dx, dy, 0, 0) for dy in (0, 2) for dx in range(NX) if dx or dy),
-        *(device(0, dy, 0, 0) for dy in (1, 3)),
-        *(device(0, 0, dz, 0) for dz in range(1, NZ)),
+        *(device(dx, 0, 0, 0) for dx in range(1, NX)),
+        *(device(0, dy, 0, 0) for dy in range(1, NY)),
+        *beside,
         device(0, 0, 0, 1),
     ]
+
+    def tell(hop):
+        for peer in beside:
+            pl.semaphore_signal(hop_sem.at[hop], inc=1, device_id=peer, device_id_type=MESH)
+
+    def heard(hop):
+        pl.semaphore_wait(hop_sem.at[hop], len(beside))
 
     loads = [
         pltpu.make_async_copy(act_hbm, act, load_sem.at[0]),
@@ -153,6 +162,7 @@
             send_inputs(kind, u)
     for u in range(UNITS):
         send_inputs(OWN_CLASS, u)
+    tell(0)
 
     def own_terms(kind, carry):
         for u in range(UNITS):
@@ -171,6 +181,8 @@
     for b in range(HALVES):
         for dx in across:
             g_copy(dx, b).wait_recv()
+        heard(b)
+        tell(b + 1)
         for u in range(UNITS):
             if b == 0:
                 for dx in across:
@@ -188,6 +200,7 @@
         return carry
 
     lax.fori_loop(0, 2 * UNITS, next_rows, 0)
+    heard(HOPS - 1)
 
     def own_node(u):
         for dx in across:
@@ -238,7 +251,7 @@
     second_now = 0.95 * second[...] + 0.05 * grad * grad
     update = first_now / (1.0 - 0.9**10) / (jnp.sqrt(second_now / (1.0 - 0.95**10)) + 1e-08)
     weight[...] = (master[...] - 0.01 * update).astype(BF16)
-    for i in reversed(range(LOCALS - 1)):
+    for i in (5, 4, 6, 3, 1, 0, 2):
         w_copy(i).start()
     weight_out[pl.ds(pl.multiple_of(local * OWN, OWN), OWN)] = weight[...]
     first_out[...] = first_now
@@ -327,6 +340,7 @@
             dma((UNITS, QUADS)),
             dma((LOCALS - 1,)),
             dma((LOCALS - 1,)),
+            pltpu.SemaphoreType.REGULAR((HOPS,)),
         ],
         compiler_params=pltpu.CompilerParams(
             collective_id=0, has_side_effects=True, vmem_limit_bytes=16 * 1024 * 1024

time: 44.3 us -> 43.2 us (0.975)
  Pallas kernels: 43.4 us -> 42.4 us
    pallas_call x1, Pallas kernels: 42.7 us -> 41.7 us  [per_device(): pl.pallas_call(kernel, out_shape=tuple((vmem(result.shape, result.dtype)...]
where the time goes in v4:
time: 43.2 us; the launch traced here: 43.1 us
  Pallas kernels  42.4 us (98%)
  between operations  0.64 us (1%)
    pallas_call x1, Pallas kernels, per_device(): pl.pallas_call(kernel, out_shape=tuple((vmem(result.shape, result.dtype)...  41.7 us

profile of v4, /device:TPU:1, one launch (start us, length us, event | category | flops | bytes accessed | tf_op | source)
XLA Modules:
  0.0 43.1 jit_solution(17448323982805376234)
XLA Ops:
  0.6 41.7 %shard_map.76 = (bf16[128,512]{1,0:T(8,128)(2,1)S(1)}, f32[16,512]{1,0:T(8,128)S(1)}, f32[16,512]{1,0:T(8,128)S(1)}) custom-call(bf16[128,4096]{1,0:T(8,128)(2,1)} %act_hbm.1, bf16[128,512]{1,0:T(8,128)(2,1)} %grads_hbm.1, f32[16,512]{1,0:T(8,128)} %master_hbm.1, f32[16,512]{1,0:T(8,128)} %first_hbm.1, f32[16,512]{1,0:T(8,128)} %second_hbm.1), custom_call_target="tpu_custom_call" | custom-call | tf_op jit(solution)/shard_map/pallas_call | solution.py:307
  42.4 0.7 %shard_map.77 = (bf16[128,512]{1,0:T(8,128)(2,1)}, f32[16,512]{1,0:T(8,128)}, f32[16,512]{1,0:T(8,128)}) custom-call(bf16[128,512]{1,0:T(8,128)(2,1)S(1)} %get-tuple-element.6.weight, f32[16,512]{1,0:T(8,128)S(1)} %get-tuple-element.7.first, f32[16,512]{1,0:T(8,128)S(1)} %get-tuple-element.8.second), custom_call_target="tpu_custom_call" | custom-call | tf_op jit(solution)/shard_map/pallas_call | solution.py:349

commit v5 on v4

--- a/solution.py
+++ b/solution.py
@@ -16,12 +16,13 @@
 TOK = 128
 COLS = 512
 HALVES = COLS // BLOCK
-UNITS = 2
-FAR = ((4, 3, 5, 2), (6, 1, 7, 0))
-QUADS = 4
+UNITS = 4
+FAR = ((4, 3), (5, 2), (6, 1), (7, 0))
+QUADS = 2
 CLASSES = 4
 STEP = (2, 1, 3, 0)
 OWN_CLASS = 3
+BOTH = tuple(range(HALVES))
 SLOTS = NCORE * QUADS
 ROWS = SLOTS * OWN
 KEEP = ROWS // NCORE
@@ -117,6 +118,12 @@
         grad = jnp.dot(inputs.reshape(ROWS, TOK), g[dx, b], preferred_element_type=F32)
         return quantize_restore(grad)
 
+    def own_terms(kind, carry):
+        for u in range(UNITS):
+            for b in range(HALVES):
+                base[kind, u, b] = ring_term(0, kind, u, b)
+        return carry
+
     pl.semaphore_wait(barrier, len(peers))
 
     def g_copy(dx, b):
@@ -128,14 +135,16 @@
             a_ss.at[dx - 1, kind, u], a_rs.at[dx - 1, kind, u], device(dx, 0, 0, 0),
         )
 
-    def y_copy(kind, step, u, b):
+    def y_copy(kind, step, u, halves):
+        part = pl.ds(halves[0], len(halves))
+        sem = u * HALVES + halves[0]
         return remote(
-            y_send.at[kind, u, b], y_recv.at[kind, u, b],
-            y_ss.at[kind, u, b], y_rs.at[kind, u, b], device(0, step, 0, 0),
+            y_send.at[kind, u, part], y_recv.at[kind, u, part],
+            y_ss.at[kind, sem], y_rs.at[kind, sem], device(0, step, 0, 0),
         )
 
-    def d_copy(u, b):
-        return remote(d_send.at[u, b], d_recv.at[u, b], d_ss.at[u, b], d_rs.at[u, b], device(0, 0, 0, 1))
+    def d_copy(u):
+        return remote(d_send.at[u], d_recv.at[u], d_ss.at[u], d_rs.at[u], device(0, 0, 0, 1))
 
     def z_copy(u, q):
         return remote(z_send.at[u, q], z_recv.at[u, q], z_ss.at[u, q], z_rs.at[u, q], device(0, 0, FAR[u][q], 0))
@@ -163,13 +172,6 @@
     for u in range(UNITS):
         send_inputs(OWN_CLASS, u)
     tell(0)
-
-    def own_terms(kind, carry):
-        for u in range(UNITS):
-            for b in range(HALVES):
-                base[kind, u, b] = ring_term(0, kind, u, b)
-        return carry
-
     lax.fori_loop(0, CLASSES, own_terms, 0)
 
     def ring_sum(kind, u, b):
@@ -188,15 +190,16 @@
                 for dx in across:
                     a_copy(dx, 0, u).wait_recv()
             y_send[0, u, b] = ring_sum(0, u, b).astype(BF16)
-            y_copy(0, STEP[0], u, b).start()
+            y_copy(0, STEP[0], u, (b,)).start()
 
     def next_rows(i, carry):
         kind, u = 1 + i % 2, i // 2
         for dx in across:
             a_copy(dx, kind, u).wait_recv()
-        for b in range(HALVES):
-            y_send[kind, u, b] = ring_sum(kind, u, b).astype(BF16)
-            y_copy(kind, 2 * kind - 1, u, b).start()
+        sums = [ring_sum(kind, u, b) for b in range(HALVES)]
+        for b in range(HALVES):
+            y_send[kind, u, b] = sums[b].astype(BF16)
+        y_copy(kind, 2 * kind - 1, u, BOTH).start()
         return carry
 
     lax.fori_loop(0, 2 * UNITS, next_rows, 0)
@@ -206,22 +209,24 @@
         for dx in across:
             a_copy(dx, OWN_CLASS, u).wait_recv()
         for b in range(HALVES):
-            y_copy(0, STEP[0], u, b).wait_recv()
-            base[OWN_CLASS, u, b] = quantize_restore(ring_sum(OWN_CLASS, u, b) + y_recv[0, u, b].astype(F32))
+            y_copy(0, STEP[0], u, (b,)).wait_recv()
+        sums = [ring_sum(OWN_CLASS, u, b) + y_recv[0, u, b].astype(F32) for b in range(HALVES)]
+        sums = [quantize_restore(total) for total in sums]
+        for b in range(HALVES):
+            base[OWN_CLASS, u, b] = sums[b]
 
     def next_node(u):
-        for b in range(HALVES):
-            for kind in (1, 2):
-                y_copy(kind, STEP[kind], u, b).wait_recv()
+        for kind in (1, 2):
+            y_copy(kind, STEP[kind], u, BOTH).wait_recv()
+        for b in range(HALVES):
             both = quantize_restore(y_recv[1, u, b].astype(F32) + y_recv[2, u, b].astype(F32))
             both = both + base[OWN_CLASS, u, b]
             keep[u, b] = both[:KEEP]
             d_send[u, b] = both[KEEP:]
-            d_copy(u, b).start()
+        d_copy(u).start()
 
     def to_owners(u):
-        for b in range(HALVES):
-            d_copy(u, b).wait_recv()
+        d_copy(u).wait_recv()
         for q in range(QUADS):
             rows = pl.ds(q * OWN, OWN)
             pair = keep[u, :, rows] + d_recv[u, :, rows]
@@ -233,12 +238,18 @@
             if FAR[u][q]:
                 z_copy(u, q).start()
 
-    own_node(0)
-    next_node(0)
-    own_node(1)
-    to_owners(0)
-    next_node(1)
-    to_owners(1)
+    for u in range(UNITS):
+        own_node(u)
+        next_node(u)
+
+        @pl.when(core == 0)
+        def _(u=u):
+            to_owners(u)
+
+    @pl.when(core == 1)
+    def _():
+        for u in range(UNITS):
+            to_owners(u)
 
     total = own_sum[...]
     for u in range(UNITS):
@@ -266,9 +277,10 @@
             for dx in across:
                 a_copy(dx, kind, u).wait_send()
         for b in range(HALVES):
-            for kind in range(OWN_CLASS):
-                y_copy(kind, STEP[kind], u, b).wait_send()
-            d_copy(u, b).wait_send()
+            y_copy(0, STEP[0], u, (b,)).wait_send()
+        for kind in (1, 2):
+            y_copy(kind, STEP[kind], u, BOTH).wait_send()
+        d_copy(u).wait_send()
         return carry
 
     lax.fori_loop(0, UNITS, drain, 0)
@@ -332,10 +344,10 @@
             dma((NX - 1, HALVES)),
             dma((NX - 1, CLASSES, UNITS)),
             dma((NX - 1, CLASSES, UNITS)),
-            dma((CLASSES - 1, UNITS, HALVES)),
-            dma((CLASSES - 1, UNITS, HALVES)),
-            dma((UNITS, HALVES)),
-            dma((UNITS, HALVES)),
+            dma((CLASSES - 1, UNITS * HALVES)),
+            dma((CLASSES - 1, UNITS * HALVES)),
+            dma((UNITS,)),
+            dma((UNITS,)),
             dma((UNITS, QUADS)),
             dma((UNITS, QUADS)),
             dma((LOCALS - 1,)),

time: 43.2 us -> 42.4 us (0.981)
  Pallas kernels: 42.4 us -> 41.7 us
    pallas_call x1, Pallas kernels: 41.7 us -> 41 us  [per_device(): pl.pallas_call(kernel, out_shape=tuple((vmem(result.shape, result.dtype)...]
where the time goes in v5:
time: 42.4 us; the launch traced here: 42.3 us
  Pallas kernels  41.7 us (98%)
  between operations  0.64 us (2%)
    pallas_call x1, Pallas kernels, per_device(): pl.pallas_call(kernel, out_shape=tuple((vmem(result.shape, result.dtype)...  41 us

profile of v5, /device:TPU:1, one launch (start us, length us, event | category | flops | bytes accessed | tf_op | source)
XLA Modules:
  0.0 42.3 jit_solution(18307639650205836577)
XLA Ops:
  0.6 41.0 %shard_map.76 = (bf16[128,512]{1,0:T(8,128)(2,1)S(1)}, f32[16,512]{1,0:T(8,128)S(1)}, f32[16,512]{1,0:T(8,128)S(1)}) custom-call(bf16[128,4096]{1,0:T(8,128)(2,1)} %act_hbm.1, bf16[128,512]{1,0:T(8,128)(2,1)} %grads_hbm.1, f32[16,512]{1,0:T(8,128)} %master_hbm.1, f32[16,512]{1,0:T(8,128)} %first_hbm.1, f32[16,512]{1,0:T(8,128)} %second_hbm.1), custom_call_target="tpu_custom_call" | custom-call | tf_op jit(solution)/shard_map/pallas_call | solution.py:319
  41.6 0.7 %shard_map.77 = (bf16[128,512]{1,0:T(8,128)(2,1)}, f32[16,512]{1,0:T(8,128)}, f32[16,512]{1,0:T(8,128)}) custom-call(bf16[128,512]{1,0:T(8,128)(2,1)S(1)} %get-tuple-element.6.weight, f32[16,512]{1,0:T(8,128)S(1)} %get-tuple-element.7.first, f32[16,512]{1,0:T(8,128)S(1)} %get-tuple-element.8.second), custom_call_target="tpu_custom_call" | custom-call | tf_op jit(solution)/shard_map/pallas_call | solution.py:361

commit v6 on v5

--- a/solution.py
+++ b/solution.py
@@ -17,11 +17,13 @@
 COLS = 512
 HALVES = COLS // BLOCK
 UNITS = 4
-FAR = ((4, 3), (5, 2), (6, 1), (7, 0))
 QUADS = 2
+LAST = NZ - 1
 CLASSES = 4
 STEP = (2, 1, 3, 0)
 OWN_CLASS = 3
+FIRST = 2
+LATER = ((1, 0), (2, 0), (3, 0), (1, 1), (2, 1), (0, 2), (0, 3), (1, 2), (2, 2), (1, 3), (2, 3), (3, 1), (3, 2), (3, 3))
 BOTH = tuple(range(HALVES))
 SLOTS = NCORE * QUADS
 ROWS = SLOTS * OWN
@@ -56,6 +58,10 @@
         to_node = ((to_y % NYLO) * NZ + (z + dz) % NZ) * NCORE + (core + dc) % NCORE
         return to_node, (to_y // NYLO) * NX + (x + dx) % NX
 
+    def away(u, q):
+        place = u * QUADS + q
+        return 0 if place == LAST else (place + (place + NZ - z) // NZ - z + NZ) % NZ
+
     def remote(src, dst, ss, rs, to):
         return pltpu.make_async_remote_copy(
             src_ref=src, dst_ref=dst, send_sem=ss, recv_sem=rs, device_id=to, device_id_type=MESH
@@ -63,8 +69,8 @@
 
     beside = [device(0, 0, 1, 0), device(0, 0, NZ - 1, 0)]
     peers = [
-        *(device(dx, 0, 0, 0) for dx in range(1, NX)),
-        *(device(0, dy, 0, 0) for dy in range(1, NY)),
+        *(device(dx, 0, 0, 0) for dx in (2, 1, 3)),
+        *(device(0, dy, 0, 0) for dy in (2, 1, 3)),
         *beside,
         device(0, 0, 0, 1),
     ]
@@ -86,11 +92,12 @@
         pltpu.make_async_copy(first_hbm, first, load_sem.at[2 + HALVES]),
         pltpu.make_async_copy(second_hbm, second, load_sem.at[3 + HALVES]),
     ]
-    for load in loads:
-        load.start()
+    loads[0].start()
     barrier = pltpu.get_barrier_semaphore()
     for peer in peers:
         pl.semaphore_signal(barrier, inc=1, device_id=peer, device_id_type=MESH)
+    for load in loads[1:]:
+        load.start()
 
     loads[0].wait()
     next_hi = ((y + 1) % NY) // NYLO
@@ -99,7 +106,7 @@
         yr, cr = i // NCORE, i % NCORE
         for u in range(UNITS):
             for q in range(QUADS):
-                m = device(0, yr, FAR[u][q], cr)[0]
+                m = device(0, yr, away(u, q), cr)[0]
                 columns = pl.ds(pl.multiple_of(m * (LOCALS * OWN), LOCALS * OWN), LOCALS * OWN)
                 turned = act[:, columns].T
                 for owner in range(LOCALS):
@@ -146,8 +153,8 @@
     def d_copy(u):
         return remote(d_send.at[u], d_recv.at[u], d_ss.at[u], d_rs.at[u], device(0, 0, 0, 1))
 
-    def z_copy(u, q):
-        return remote(z_send.at[u, q], z_recv.at[u, q], z_ss.at[u, q], z_rs.at[u, q], device(0, 0, FAR[u][q], 0))
+    def z_copy(u, q, dz):
+        return remote(z_send.at[u, q], z_recv.at[dz], z_ss.at[u, q], z_rs.at[dz], device(0, 0, dz, 0))
 
     def w_copy(i):
         dy, dx = 2 * ((i + 1) // NX), (i + 1) % NX
@@ -162,15 +169,12 @@
 
     for dx in across:
         g_copy(dx, 0).start()
-    for u in range(UNITS):
+    for u in range(FIRST):
         send_inputs(0, u)
     for dx in across:
         g_copy(dx, 1).start()
-    for u in range(UNITS):
-        for kind in (1, 2):
-            send_inputs(kind, u)
-    for u in range(UNITS):
-        send_inputs(OWN_CLASS, u)
+    for kind, u in LATER:
+        send_inputs(kind, u)
     tell(0)
     lax.fori_loop(0, CLASSES, own_terms, 0)
 
@@ -180,18 +184,20 @@
             total = total + ring_term(dx, kind, u, b)
         return total
 
+    def first_rows(u, b):
+        y_send[0, u, b] = ring_sum(0, u, b).astype(BF16)
+        y_copy(0, STEP[0], u, (b,)).start()
+
     for b in range(HALVES):
         for dx in across:
             g_copy(dx, b).wait_recv()
         heard(b)
         tell(b + 1)
-        for u in range(UNITS):
+        for u in range(FIRST):
             if b == 0:
                 for dx in across:
                     a_copy(dx, 0, u).wait_recv()
-            y_send[0, u, b] = ring_sum(0, u, b).astype(BF16)
-            y_copy(0, STEP[0], u, (b,)).start()
-
+            first_rows(u, b)
     def next_rows(i, carry):
         kind, u = 1 + i % 2, i // 2
         for dx in across:
@@ -202,7 +208,13 @@
         y_copy(kind, 2 * kind - 1, u, BOTH).start()
         return carry
 
-    lax.fori_loop(0, 2 * UNITS, next_rows, 0)
+    lax.fori_loop(0, 2 * FIRST, next_rows, 0)
+    for u in range(FIRST, UNITS):
+        for dx in across:
+            a_copy(dx, 0, u).wait_recv()
+        for b in range(HALVES):
+            first_rows(u, b)
+    lax.fori_loop(2 * FIRST, 2 * UNITS - 2, next_rows, 0)
     heard(HOPS - 1)
 
     def own_node(u):
@@ -231,12 +243,12 @@
             rows = pl.ds(q * OWN, OWN)
             pair = keep[u, :, rows] + d_recv[u, :, rows]
             for b in range(HALVES):
-                if FAR[u][q] == 0:
+                if u * QUADS + q == LAST:
                     own_sum[:, b * BLOCK : (b + 1) * BLOCK] = pair[b]
                 else:
                     z_send[u, q, :, b * BLOCK : (b + 1) * BLOCK] = pair[b].astype(BF16)
-            if FAR[u][q]:
-                z_copy(u, q).start()
+            if u * QUADS + q != LAST:
+                z_copy(u, q, away(u, q)).start()
 
     for u in range(UNITS):
         own_node(u)
@@ -246,17 +258,22 @@
         def _(u=u):
             to_owners(u)
 
+        if u == 0:
+            lax.fori_loop(2 * UNITS - 2, 2 * UNITS, next_rows, 0)
+        if u == 2:
+            @pl.when(core == 1)
+            def _():
+                to_owners(0)
+
     @pl.when(core == 1)
     def _():
-        for u in range(UNITS):
+        for u in range(1, UNITS):
             to_owners(u)
 
     total = own_sum[...]
-    for u in range(UNITS):
-        for q in range(QUADS):
-            if FAR[u][q]:
-                z_copy(u, q).wait_recv()
-                total = total + z_recv[u, q].astype(F32)
+    for dz in range(1, NZ):
+        z_copy(0, 0, dz).wait_recv()
+        total = total + z_recv[dz].astype(F32)
     grad = total / (NODES * LOCALS)
     first_now = 0.9 * first[...] + 0.1 * grad
     second_now = 0.95 * second[...] + 0.05 * grad * grad
@@ -286,8 +303,8 @@
     lax.fori_loop(0, UNITS, drain, 0)
     for u in range(UNITS):
         for q in range(QUADS):
-            if FAR[u][q]:
-                z_copy(u, q).wait_send()
+            if u * QUADS + q != LAST:
+                z_copy(u, q, away(u, q)).wait_send()
     for i in range(LOCALS - 1):
         w_copy(i).wait_send()
     for i in range(LOCALS - 1):
@@ -333,7 +350,7 @@
             vmem((UNITS, HALVES, KEEP, BLOCK), F32),
             vmem((UNITS, HALVES, KEEP, BLOCK), F32),
             vmem((UNITS, QUADS, OWN, COLS), BF16),
-            vmem((UNITS, QUADS, OWN, COLS), BF16),
+            vmem((NZ, OWN, COLS), BF16),
             vmem((OWN, COLS), F32),
             vmem((OWN, COLS), F32),
             vmem((OWN, COLS), F32),
@@ -349,7 +366,7 @@
             dma((UNITS,)),
             dma((UNITS,)),
             dma((UNITS, QUADS)),
-            dma((UNITS, QUADS)),
+            dma((NZ,)),
             dma((LOCALS - 1,)),
             dma((LOCALS - 1,)),
             pltpu.SemaphoreType.REGULAR((HOPS,)),

time: 42.4 us -> 40.5 us (0.955)
  Pallas kernels: 41.7 us -> 39.8 us
    pallas_call x1, Pallas kernels: 41 us -> 39.1 us  [per_device(): pl.pallas_call(kernel, out_shape=tuple((vmem(result.shape, result.dtype)...]
where the time goes in v6:
time: 40.5 us; the launch traced here: 40.4 us
  Pallas kernels  39.8 us (98%)
  between operations  0.64 us (2%)
    pallas_call x1, Pallas kernels, per_device(): pl.pallas_call(kernel, out_shape=tuple((vmem(result.shape, result.dtype)...  39.1 us

profile of v6, /device:TPU:1, one launch (start us, length us, event | category | flops | bytes accessed | tf_op | source)
XLA Modules:
  0.0 40.4 jit_solution(12906816034001487118)
XLA Ops:
  0.6 39.1 %shard_map.76 = (bf16[128,512]{1,0:T(8,128)(2,1)S(1)}, f32[16,512]{1,0:T(8,128)S(1)}, f32[16,512]{1,0:T(8,128)S(1)}) custom-call(bf16[128,4096]{1,0:T(8,128)(2,1)} %act_hbm.1, bf16[128,512]{1,0:T(8,128)(2,1)} %grads_hbm.1, f32[16,512]{1,0:T(8,128)} %master_hbm.1, f32[16,512]{1,0:T(8,128)} %first_hbm.1, f32[16,512]{1,0:T(8,128)} %second_hbm.1), custom_call_target="tpu_custom_call" | custom-call | tf_op jit(solution)/shard_map/pallas_call | solution.py:336
  39.7 0.7 %shard_map.77 = (bf16[128,512]{1,0:T(8,128)(2,1)}, f32[16,512]{1,0:T(8,128)}, f32[16,512]{1,0:T(8,128)}) custom-call(bf16[128,512]{1,0:T(8,128)(2,1)S(1)} %get-tuple-element.6.weight, f32[16,512]{1,0:T(8,128)S(1)} %get-tuple-element.7.first, f32[16,512]{1,0:T(8,128)S(1)} %get-tuple-element.8.second), custom_call_target="tpu_custom_call" | custom-call | tf_op jit(solution)/shard_map/pallas_call | solution.py:378

commit v7 on v6

--- a/solution.py
+++ b/solution.py
@@ -28,7 +28,7 @@
 SLOTS = NCORE * QUADS
 ROWS = SLOTS * OWN
 KEEP = ROWS // NCORE
-HOPS = NZ // 2 - 1
+REACH = (1, 2, 4)
 
 
 def quantize_restore(values):
@@ -67,20 +67,28 @@
             src_ref=src, dst_ref=dst, send_sem=ss, recv_sem=rs, device_id=to, device_id_type=MESH
         )
 
-    beside = [device(0, 0, 1, 0), device(0, 0, NZ - 1, 0)]
     peers = [
-        *(device(dx, 0, 0, 0) for dx in (2, 1, 3)),
-        *(device(0, dy, 0, 0) for dy in (2, 1, 3)),
-        *beside,
+        *(device(dx, 0, 0, 0) for dx in range(1, NX)),
+        *(device(0, dy, 0, 0) for dy in range(1, NY)),
         device(0, 0, 0, 1),
     ]
+    def along(d):
+        return (z + NZ - d) // NZ + 1 - (z + d) // NZ
+
+    def signal_along(sem, d):
+        @pl.when(z < NZ - d)
+        def _():
+            pl.semaphore_signal(sem, inc=1, device_id=device(0, 0, d, 0), device_id_type=MESH)
+
+        @pl.when(z >= d)
+        def _():
+            pl.semaphore_signal(sem, inc=1, device_id=device(0, 0, NZ - d, 0), device_id_type=MESH)
 
     def tell(hop):
-        for peer in beside:
-            pl.semaphore_signal(hop_sem.at[hop], inc=1, device_id=peer, device_id_type=MESH)
+        signal_along(hop_sem.at[hop], REACH[hop])
 
     def heard(hop):
-        pl.semaphore_wait(hop_sem.at[hop], len(beside))
+        pl.semaphore_wait(hop_sem.at[hop], along(REACH[hop]))
 
     loads = [
         pltpu.make_async_copy(act_hbm, act, load_sem.at[0]),
@@ -96,6 +104,7 @@
     barrier = pltpu.get_barrier_semaphore()
     for peer in peers:
         pl.semaphore_signal(barrier, inc=1, device_id=peer, device_id_type=MESH)
+    signal_along(barrier, 1)
     for load in loads[1:]:
         load.start()
 
@@ -131,7 +140,7 @@
                 base[kind, u, b] = ring_term(0, kind, u, b)
         return carry
 
-    pl.semaphore_wait(barrier, len(peers))
+    pl.semaphore_wait(barrier, len(peers) + along(1))
 
     def g_copy(dx, b):
         return remote(g.at[0, b], g.at[dx, b], g_ss.at[dx - 1, b], g_rs.at[dx - 1, b], device(dx, 0, 0, 0))
@@ -214,8 +223,6 @@
             a_copy(dx, 0, u).wait_recv()
         for b in range(HALVES):
             first_rows(u, b)
-    lax.fori_loop(2 * FIRST, 2 * UNITS - 2, next_rows, 0)
-    heard(HOPS - 1)
 
     def own_node(u):
         for dx in across:
@@ -252,22 +259,25 @@
 
     for u in range(UNITS):
         own_node(u)
+        if u >= 2:
+            @pl.when(core == 1)
+            def _(u=u):
+                to_owners(u - 2)
+
         next_node(u)
+        if u == 0:
+            heard(2)
 
         @pl.when(core == 0)
         def _(u=u):
             to_owners(u)
 
         if u == 0:
-            lax.fori_loop(2 * UNITS - 2, 2 * UNITS, next_rows, 0)
-        if u == 2:
-            @pl.when(core == 1)
-            def _():
-                to_owners(0)
+            lax.fori_loop(2 * FIRST, 2 * UNITS, next_rows, 0)
 
     @pl.when(core == 1)
     def _():
-        for u in range(1, UNITS):
+        for u in range(2, UNITS):
             to_owners(u)
 
     total = own_sum[...]
@@ -369,7 +379,7 @@
             dma((NZ,)),
             dma((LOCALS - 1,)),
             dma((LOCALS - 1,)),
-            pltpu.SemaphoreType.REGULAR((HOPS,)),
+            pltpu.SemaphoreType.REGULAR((len(REACH),)),
         ],
         compiler_params=pltpu.CompilerParams(
             collective_id=0, has_side_effects=True, vmem_limit_bytes=16 * 1024 * 1024

time: 40.5 us -> 39.5 us (0.975)
  Pallas kernels: 39.8 us -> 38.6 us
    pallas_call x1, Pallas kernels: 39.1 us -> 37.9 us  [per_device(): pl.pallas_call(kernel, out_shape=tuple((vmem(result.shape, result.dtype)...]
where the time goes in v7:
time: 39.5 us; the launch traced here: 39.3 us
  Pallas kernels  38.6 us (98%)
  between operations  0.64 us (2%)
    pallas_call x1, Pallas kernels, per_device(): pl.pallas_call(kernel, out_shape=tuple((vmem(result.shape, result.dtype)...  37.9 us

profile of v7, /device:TPU:1, one launch (start us, length us, event | category | flops | bytes accessed | tf_op | source)
XLA Modules:
  0.0 39.3 jit_solution(2188458069273246914)
XLA Ops:
  0.6 37.9 %shard_map.76 = (bf16[128,512]{1,0:T(8,128)(2,1)S(1)}, f32[16,512]{1,0:T(8,128)S(1)}, f32[16,512]{1,0:T(8,128)S(1)}) custom-call(bf16[128,4096]{1,0:T(8,128)(2,1)} %act_hbm.1, bf16[128,512]{1,0:T(8,128)(2,1)} %grads_hbm.1, f32[16,512]{1,0:T(8,128)} %master_hbm.1, f32[16,512]{1,0:T(8,128)} %first_hbm.1, f32[16,512]{1,0:T(8,128)} %second_hbm.1), custom_call_target="tpu_custom_call" | custom-call | tf_op jit(solution)/shard_map/pallas_call | solution.py:346
  38.6 0.7 %shard_map.77 = (bf16[128,512]{1,0:T(8,128)(2,1)}, f32[16,512]{1,0:T(8,128)}, f32[16,512]{1,0:T(8,128)}) custom-call(bf16[128,512]{1,0:T(8,128)(2,1)S(1)} %get-tuple-element.6.weight, f32[16,512]{1,0:T(8,128)S(1)} %get-tuple-element.7.first, f32[16,512]{1,0:T(8,128)S(1)} %get-tuple-element.8.second), custom_call_target="tpu_custom_call" | custom-call | tf_op jit(solution)/shard_map/pallas_call | solution.py:388

commit v8 on v7

--- a/solution.py
+++ b/solution.py
@@ -170,7 +170,7 @@
         mine = pl.ds(pl.multiple_of(local * OWN, OWN), OWN)
         return remote(weight, weight_out.at[mine], w_ss.at[i], w_rs.at[i], device(dx, dy, 0, 0))
 
-    across = (1, 3, 2)
+    across = (2, 1, 3)
 
     def send_inputs(kind, u):
         for dx in across:

time: 39.5 us -> 39.2 us (level)
  no operation moved by 1% of the time
where the time goes in v8:
time: 39.2 us; the launch traced here: 39 us
  Pallas kernels  38.3 us (98%)
  between operations  0.64 us (2%)
    pallas_call x1, Pallas kernels, per_device(): pl.pallas_call(kernel, out_shape=tuple((vmem(result.shape, result.dtype)...  37.6 us

profile of v8, /device:TPU:1, one launch (start us, length us, event | category | flops | bytes accessed | tf_op | source)
XLA Modules:
  0.0 39.0 jit_solution(7399083041401942498)
XLA Ops:
  0.6 37.6 %shard_map.76 = (bf16[128,512]{1,0:T(8,128)(2,1)S(1)}, f32[16,512]{1,0:T(8,128)S(1)}, f32[16,512]{1,0:T(8,128)S(1)}) custom-call(bf16[128,4096]{1,0:T(8,128)(2,1)} %act_hbm.1, bf16[128,512]{1,0:T(8,128)(2,1)} %grads_hbm.1, f32[16,512]{1,0:T(8,128)} %master_hbm.1, f32[16,512]{1,0:T(8,128)} %first_hbm.1, f32[16,512]{1,0:T(8,128)} %second_hbm.1), custom_call_target="tpu_custom_call" | custom-call | tf_op jit(solution)/shard_map/pallas_call | solution.py:346
  38.3 0.7 %shard_map.77 = (bf16[128,512]{1,0:T(8,128)(2,1)}, f32[16,512]{1,0:T(8,128)}, f32[16,512]{1,0:T(8,128)}) custom-call(bf16[128,512]{1,0:T(8,128)(2,1)S(1)} %get-tuple-element.6.weight, f32[16,512]{1,0:T(8,128)S(1)} %get-tuple-element.7.first, f32[16,512]{1,0:T(8,128)S(1)} %get-tuple-element.8.second), custom_call_target="tpu_custom_call" | custom-call | tf_op jit(solution)/shard_map/pallas_call | solution.py:388

commit v9 on v8

--- a/solution.py
+++ b/solution.py
@@ -68,8 +68,8 @@
         )
 
     peers = [
-        *(device(dx, 0, 0, 0) for dx in range(1, NX)),
-        *(device(0, dy, 0, 0) for dy in range(1, NY)),
+        *(device(dx, 0, 0, 0) for dx in (2, 1, 3)),
+        *(device(0, dy, 0, 0) for dy in (2, 1, 3)),
         device(0, 0, 0, 1),
     ]
     def along(d):

time: 39.2 us -> 39.2 us (level)
  no operation moved by 1% of the time
where the time goes in v9:
time: 39.2 us; the launch traced here: 39 us
  Pallas kernels  38.3 us (98%)
  between operations  0.64 us (2%)
    pallas_call x1, Pallas kernels, per_device(): pl.pallas_call(kernel, out_shape=tuple((vmem(result.shape, result.dtype)...  37.6 us

profile of v9, /device:TPU:1, one launch (start us, length us, event | category | flops | bytes accessed | tf_op | source)
XLA Modules:
  0.0 39.0 jit_solution(18298829603071657897)
XLA Ops:
  0.6 37.6 %shard_map.76 = (bf16[128,512]{1,0:T(8,128)(2,1)S(1)}, f32[16,512]{1,0:T(8,128)S(1)}, f32[16,512]{1,0:T(8,128)S(1)}) custom-call(bf16[128,4096]{1,0:T(8,128)(2,1)} %act_hbm.1, bf16[128,512]{1,0:T(8,128)(2,1)} %grads_hbm.1, f32[16,512]{1,0:T(8,128)} %master_hbm.1, f32[16,512]{1,0:T(8,128)} %first_hbm.1, f32[16,512]{1,0:T(8,128)} %second_hbm.1), custom_call_target="tpu_custom_call" | custom-call | tf_op jit(solution)/shard_map/pallas_call | solution.py:346
  38.3 0.7 %shard_map.77 = (bf16[128,512]{1,0:T(8,128)(2,1)}, f32[16,512]{1,0:T(8,128)}, f32[16,512]{1,0:T(8,128)}) custom-call(bf16[128,512]{1,0:T(8,128)(2,1)S(1)} %get-tuple-element.6.weight, f32[16,512]{1,0:T(8,128)S(1)} %get-tuple-element.7.first, f32[16,512]{1,0:T(8,128)S(1)} %get-tuple-element.8.second), custom_call_target="tpu_custom_call" | custom-call | tf_op jit(solution)/shard_map/pallas_call | solution.py:388
